TPU v7x, 32 devices: a whole 2x2x4 slice. The times are simulated.
32 devices in a mesh: patch: 8 (over z, y), sub: 4 (over x, core).
Axes of the slice: x: 2, y: 2, z: 4, core: 2. Of those that a mesh axis runs over, the one named last changes fastest.
Arguments:
- sources: int32 [128, 2], replicated, may hold values from 0 to 16383
- diag_coef: float32 [16384], P(('patch', 'sub')), may hold values from 1 to 2
- tiles: float32 [128, 6, 128, 128], P(('patch', 'sub')), may hold values from -0.109375 to 0.109375
- tile_cols: int32 [128, 6], P(('patch', 'sub')), may hold values from 0 to 7
- send_rows: int32 [32, 4, 128], P(('patch', 'sub')), may hold values from 0 to 511
- recv_rows: int32 [32, 512], P(('patch', 'sub')), may hold values from 0 to 511, each once within a row
- bounds: float32 [2], replicated, may hold values from 0.3 to 3.2, as said below
Outputs:
- solution: float32 [16384, 128], P(('patch', 'sub'))
- res_norm: float32 [128], replicated
Inputs may be any that keep to these rules, and one draw needn't show every extreme that they name: bounds[0] lies in 0.3 to 0.5 and bounds[1] in 2.6 to 3.2.
All inputs are finite; a program needn't handle non-finite values.
Results may differ from a plain program's by a relative error of at most 0.0001.
Values sent between devices are 32-bit elements; how exact they have to be, the bound alone decides.
A program may use at most 64 MiB of HBM per device.

v0:
```python
import functools

import jax
import jax.numpy as jnp
from jax import lax
from jax.experimental import pallas as pl
from jax.experimental.pallas import tpu as pltpu
from jax.sharding import PartitionSpec as P

ITERS = 8
MESH = pl.DeviceIdType.MESH
F32 = jnp.float32
BF16 = jnp.bfloat16


def halves(value):
    high = value.astype(BF16)
    return high, (value - high.astype(F32)).astype(BF16)


def product(high, low, pair, columns):
    wide = jnp.dot(high, pair, preferred_element_type=F32)
    narrow = jnp.dot(low, pair[:, :columns], preferred_element_type=F32)
    return wide[:, :columns] + wide[:, columns:] + narrow


def kernel(
    n_patch, n_sub,
    sources_ref, diag_ref, tiles_hbm, cols_ref, sends_ref, receives_ref, bounds_ref,
    solution_ref, norm_ref,
    tiles_ref, near_hi, near_lo, far_hi, far_lo, halo_hi, halo_lo,
    direction_ref, residual_ref, packed_residual, total_ref, pair_ref, heard_pair,
    packed_ref, heard_ref, heard_rows, norms_ref, counts_ref, pick_ref, place_ref,
    message_ref, echo_out, echo_in, echo_hi, echo_lo, echo_sems,
    tile_sems, row_send, row_recv, send_sems, recv_sems, norm_send, norm_recv,
):
    blk_rows, per_row, size, _ = tiles_hbm.shape
    rows = blk_rows * size
    n_src, columns = sources_ref.shape
    sent = sends_ref.shape[2]
    halo = receives_ref.shape[1]
    packed_rows = 4 * sent
    patch, sub = lax.axis_index("patch"), lax.axis_index("sub")
    devices = n_patch * n_sub
    me = patch * n_sub + sub

    copies = [
        pltpu.make_async_copy(tiles_hbm.at[b], tiles_ref.at[b], tile_sems.at[b])
        for b in range(blk_rows)
    ]
    for copy in copies:
        copy.start()

    barrier = pltpu.get_barrier_semaphore()

    @pl.loop(1, devices)
    def _(step):
        other = lax.rem(me + step, devices)
        pl.semaphore_signal(
            barrier, inc=1, device_id=(other // n_sub, lax.rem(other, n_sub)), device_id_type=MESH
        )

    lower_patch = lax.rem(patch + n_patch - 1, n_patch)
    upper_patch = lax.rem(patch + 1, n_patch)
    lower_sub = lax.rem(sub + n_sub - 1, n_sub)
    upper_sub = lax.rem(sub + 1, n_sub)
    targets = [(lower_patch, sub), (upper_patch, sub), (patch, lower_sub), (patch, upper_sub)]
    lands = [1, 0, 3, 2]
    origins = [targets[0], targets[1], targets[2], targets[3]]

    low_end = jnp.full((1, columns), bounds_ref[0], F32)
    high_end = jnp.full((1, columns), bounds_ref[1], F32)
    centre = (low_end + high_end) / 2.0
    half_width = (high_end - low_end) / 2.0
    ratio = centre / half_width

    def counted(ids):
        total = jnp.zeros(ids.shape, F32)
        for s in range(n_src):
            total = total + jnp.where(sources_ref[s : s + 1, :] == ids, 1.0, 0.0)
        return total

    right_side = counted(me * rows + lax.broadcasted_iota(jnp.int32, (rows, columns), 0))
    counts_ref[...] = right_side

    def as_column(row, width):
        return jnp.broadcast_to(row, (width, row.shape[1])).T

    picks = []
    for j in range(4):
        wide = as_column(sends_ref[j], rows)
        picks.append(
            jnp.where(wide == lax.broadcasted_iota(jnp.int32, (sent, rows), 1), 1.0, 0.0).astype(BF16)
        )
    pick_ref[...] = jnp.concatenate(picks, axis=0)
    for i in range(halo // size):
        wide = as_column(receives_ref[:, i * size : (i + 1) * size], packed_rows)
        place_ref[pl.ds(i * size, size)] = jnp.where(
            wide == lax.broadcasted_iota(jnp.int32, (size, packed_rows), 1), 1.0, 0.0
        ).astype(BF16)

    pl.semaphore_wait(barrier, devices - 1)
    row_copies = []
    for j in range(4):
        copy = pltpu.make_async_remote_copy(
            src_ref=sends_ref.at[j], dst_ref=heard_rows.at[lands[j]],
            send_sem=row_send.at[j], recv_sem=row_recv.at[lands[j]],
            device_id=targets[j], device_id_type=MESH,
        )
        copy.start()
        row_copies.append(copy)

    eye = lax.broadcasted_iota(jnp.int32, (size, size), 0) == lax.broadcasted_iota(
        jnp.int32, (size, size), 1
    )
    for b in range(blk_rows):
        copies[b].wait()
        for c in range(blk_rows + halo // size):
            block = jnp.zeros((size, size), F32)
            for n in range(per_row):
                block = block + tiles_ref[b, n] * (cols_ref[b, n] == c).astype(F32)
            if c == b:
                block = block + jnp.where(eye, diag_ref[b : b + 1, :], 0.0)
            high, low = halves(block)
            at = pl.ds(packed_rows + b * size, size)
            if c < blk_rows:
                near_hi[at, pl.ds(c * size, size)] = high
                near_lo[at, pl.ds(c * size, size)] = low
            else:
                place_at = pl.ds((c - blk_rows) * size, size)
                halo_hi[pl.ds(b * size, size), place_at] = high
                halo_lo[pl.ds(b * size, size), place_at] = low
    own = pl.ds(packed_rows, rows)
    first = pl.ds(0, packed_rows)

    heard_counts = []
    for j in range(4):
        row_copies[j].wait()
    for j in range(4):
        base = (origins[j][0] * n_sub + origins[j][1]) * rows
        heard_counts.append(counted(base + as_column(heard_rows[j], columns)).astype(BF16))
    halo_counts = jnp.dot(
        place_ref[...], jnp.concatenate(heard_counts, axis=0), preferred_element_type=F32
    ).astype(BF16)

    def exchange(slot, j):
        return pltpu.make_async_remote_copy(
            src_ref=packed_ref.at[slot, j], dst_ref=heard_ref.at[slot, lands[j]],
            send_sem=send_sems.at[slot, j], recv_sem=recv_sems.at[slot, lands[j]],
            device_id=targets[j], device_id_type=MESH,
        )

    def arrival(slot, j):
        return pltpu.make_async_remote_copy(
            src_ref=packed_ref.at[slot, j], dst_ref=heard_ref.at[slot, j],
            send_sem=send_sems.at[slot, j], recv_sem=recv_sems.at[slot, j],
            device_id=targets[0], device_id_type=MESH,
        )

    patch_part, sub_part = pl.ds(0, 2 * sent), pl.ds(2 * sent, 2 * sent)

    def listen(slot, pieces):
        for j in pieces:
            arrival(slot, j).wait_recv()
            high, low = halves(heard_ref[slot, j])
            heard_pair[pl.ds(j * sent, sent), :columns] = high
            heard_pair[pl.ds(j * sent, sent), columns:] = low

    def far_product(at, part):
        return product(far_hi[at, part], far_lo[at, part], heard_pair[part], columns)

    def advance(damping):
        damping_next = 1.0 / (2.0 * ratio - damping)
        return damping_next, damping_next * damping, 2.0 * damping_next / half_width

    distant = lax.rem(patch, 2)
    close = 1 - distant
    distant_part = pl.ds(pl.multiple_of(distant * sent, sent), sent)
    close_part = pl.ds(pl.multiple_of(close * sent, sent), sent)

    def patch_copy(source, slot, j):
        return pltpu.make_async_remote_copy(
            src_ref=source, dst_ref=heard_ref.at[slot, 1 - j],
            send_sem=send_sems.at[slot, j], recv_sem=recv_sems.at[slot, 1 - j],
            device_id=(lax.rem(patch + n_patch + 2 * j - 1, n_patch), sub), device_id_type=MESH,
        )

    def step(slot, damping, gain_before, last):
        at = own if last else pl.ds(0, packed_rows + rows)
        total_ref[at] = product(near_hi[at], near_lo[at], pair_ref[...], columns)
        high, low = halves(packed_ref[slot - 1, distant])
        echo = gain_before * product(
            echo_hi[...], echo_lo[...], jnp.concatenate([high, low], axis=1), columns
        )
        listen(slot, (2, 3))
        total_ref[at] = total_ref[at] + far_product(at, sub_part)
        arrival(slot, close).wait_recv()
        high, low = halves(heard_ref[slot, close])
        heard_pair[close_part, :columns] = high
        heard_pair[close_part, columns:] = low
        if not last:
            damping_next, keep, gain = advance(damping)
            total = total_ref[distant_part] + far_product(distant_part, close_part)
            message_ref[slot + 1] = keep * packed_ref[slot, distant] + gain * (
                packed_residual[distant_part] - total
            )
            patch_copy(message_ref.at[slot + 1], slot + 1, distant).start()
        arrival(slot, distant).wait_recv()
        high, low = halves(heard_ref[slot, distant] - echo)
        heard_pair[distant_part, :columns] = high
        heard_pair[distant_part, columns:] = low
        if last:
            residual_ref[...] = residual_ref[...] - (total_ref[own] + far_product(own, patch_part))
            return
        for group in (0, 2):
            span = pl.ds(group * sent, 2 * sent)
            rest = packed_residual[span] - (total_ref[span] + far_product(span, patch_part))
            packed_residual[span] = rest
            for i in range(2):
                packed_ref[slot + 1, group + i] = (
                    keep * packed_ref[slot, group + i] + gain * rest[i * sent : (i + 1) * sent]
                )
            if group == 0:
                patch_copy(packed_ref.at[slot + 1, close], slot + 1, close).start()
            else:
                exchange(slot + 1, 2).start()
                exchange(slot + 1, 3).start()
        residual = residual_ref[...] - (total_ref[own] + far_product(own, patch_part))
        residual_ref[...] = residual
        direction = keep * direction_ref[...] + gain * residual
        direction_ref[...] = direction
        solution_ref[...] = solution_ref[...] + direction
        high, low = halves(direction)
        pair_ref[:, :columns] = high
        pair_ref[:, columns:] = low
        return damping_next, gain

    counts = counts_ref[...].astype(BF16)
    product_sum = (
        jnp.dot(near_hi[own], counts, preferred_element_type=F32)
        + jnp.dot(near_lo[own], counts, preferred_element_type=F32)
        + jnp.dot(halo_hi[...], halo_counts, preferred_element_type=F32)
        + jnp.dot(halo_lo[...], halo_counts, preferred_element_type=F32)
    )
    right_side = counts_ref[...]
    residual = right_side - product_sum / centre
    damping, keep, gain = advance(1.0 / ratio)
    before = right_side / centre
    direction = keep * before + gain * residual
    high, low = halves(direction)
    pair_ref[:, :columns] = high
    pair_ref[:, columns:] = low
    for group in (0, 2):
        wide = jnp.dot(
            pick_ref[pl.ds(group * sent, 2 * sent)], pair_ref[...], preferred_element_type=F32
        )
        wide = wide[:, :columns] + wide[:, columns:]
        for i in range(2):
            packed_ref[1, group + i] = wide[i * sent : (i + 1) * sent]
            exchange(1, group + i).start()
    residual_ref[...] = residual
    direction_ref[...] = direction
    solution_ref[...] = before + direction
    high, low = halves(residual)
    wide = jnp.dot(pick_ref[...], jnp.concatenate([high, low], axis=1), preferred_element_type=F32)
    packed_residual[...] = wide[:, :columns] + wide[:, columns:]

    for halo_part, far, near in ((halo_hi, far_hi, near_hi), (halo_lo, far_lo, near_lo)):
        far[own] = jnp.dot(
            halo_part[...], place_ref[...], preferred_element_type=F32
        ).astype(BF16)
        far[first] = jnp.dot(pick_ref[...], far[own], preferred_element_type=F32).astype(BF16)
        near[first] = jnp.dot(pick_ref[...], near[own], preferred_element_type=F32).astype(BF16)

    echo_out[...] = far_hi[distant_part, distant_part].astype(F32) + far_lo[
        distant_part, distant_part
    ].astype(F32)
    echo_copy = pltpu.make_async_remote_copy(
        src_ref=echo_out, dst_ref=echo_in, send_sem=echo_sems.at[0], recv_sem=echo_sems.at[1],
        device_id=(lax.rem(patch + n_patch + 2 * distant - 1, n_patch), sub), device_id_type=MESH,
    )
    echo_copy.start()
    for j in range(2):
        packed_ref[0, j] = jnp.zeros((sent, columns), F32)
    echo_hi[...] = jnp.zeros((sent, sent), BF16)
    echo_lo[...] = jnp.zeros((sent, sent), BF16)
    state = step(1, damping, jnp.zeros((1, columns), F32), False)
    echo_copy.wait()
    echo_hi[...], echo_lo[...] = halves(echo_in[...])
    damping, gain = lax.fori_loop(2, ITERS - 1, lambda k, state: step(k, *state, False), state)
    step(ITERS - 1, damping, gain, True)

    final = residual_ref[...]
    norms_ref[me] = jnp.sum(final * final, axis=0, keepdims=True)

    @pl.loop(1, devices)
    def _(step):
        other = lax.rem(me + step, devices)
        pltpu.make_async_remote_copy(
            src_ref=norms_ref.at[me], dst_ref=norms_ref.at[me],
            send_sem=norm_send, recv_sem=norm_recv,
            device_id=(other // n_sub, lax.rem(other, n_sub)), device_id_type=MESH,
        ).start()

    for slot in range(1, ITERS):
        for j in range(4):
            exchange(slot, j).wait_send()
    others = norms_ref.at[pl.ds(0, devices - 1)]
    pltpu.make_async_copy(others, others, norm_recv).wait()
    pltpu.make_async_copy(others, others, norm_send).wait()
    norm_ref[...] = norms_ref[...]


def finish(solution_ref, norms_ref, result_ref, norm_ref):
    result_ref[...] = solution_ref[...]
    norm_ref[...] = jnp.sqrt(jnp.sum(norms_ref[...], axis=0))


def solution(mesh):
    n_patch, n_sub = mesh.shape["patch"], mesh.shape["sub"]

    def on_device(sources, diag_coef, tiles, tile_cols, send_rows, recv_rows, bounds):
        blk_rows, per_row, size, _ = tiles.shape
        rows = diag_coef.shape[0]
        columns = sources.shape[0]
        sent = send_rows.shape[2]
        halo = recv_rows.shape[1]
        every = 4 * sent + rows
        vmem, smem = pltpu.VMEM, pltpu.SMEM
        held, norms = pl.pallas_call(
            functools.partial(kernel, n_patch, n_sub),
            out_shape=(
                jax.ShapeDtypeStruct((rows, columns), F32),
                jax.ShapeDtypeStruct((n_patch * n_sub, 1, columns), F32),
            ),
            in_specs=[
                pl.BlockSpec(memory_space=vmem),
                pl.BlockSpec(memory_space=vmem),
                pl.BlockSpec(memory_space=pl.ANY),
                pl.BlockSpec(memory_space=smem),
                pl.BlockSpec(memory_space=vmem),
                pl.BlockSpec(memory_space=vmem),
                pl.BlockSpec(memory_space=smem),
            ],
            out_specs=(pl.BlockSpec(memory_space=vmem), pl.BlockSpec(memory_space=vmem)),
            scratch_shapes=[
                vmem(tiles.shape, F32),
                vmem((every, rows), BF16),
                vmem((every, rows), BF16),
                vmem((every, halo), BF16),
                vmem((every, halo), BF16),
                vmem((rows, halo), BF16),
                vmem((rows, halo), BF16),
                vmem((rows, columns), F32),
                vmem((rows, columns), F32),
                vmem((4 * sent, columns), F32),
                vmem((every, columns), F32),
                vmem((rows, 2 * columns), BF16),
                vmem((4 * sent, 2 * columns), BF16),
                vmem((ITERS, 4, sent, columns), F32),
                vmem((ITERS, 4, sent, columns), F32),
                vmem((4, 1, sent), jnp.int32),
                vmem((n_patch * n_sub, 1, columns), F32),
                vmem((rows, columns), F32),
                vmem((4 * sent, rows), BF16),
                vmem((halo, 4 * sent), BF16),
                vmem((ITERS, sent, columns), F32),
                vmem((sent, sent), F32),
                vmem((sent, sent), F32),
                vmem((sent, sent), BF16),
                vmem((sent, sent), BF16),
                pltpu.SemaphoreType.DMA((2,)),
                pltpu.SemaphoreType.DMA((blk_rows,)),
                pltpu.SemaphoreType.DMA((4,)),
                pltpu.SemaphoreType.DMA((4,)),
                pltpu.SemaphoreType.DMA((ITERS, 4)),
                pltpu.SemaphoreType.DMA((ITERS, 4)),
                pltpu.SemaphoreType.DMA,
                pltpu.SemaphoreType.DMA,
            ],
            compiler_params=pltpu.CompilerParams(collective_id=0, has_side_effects=True),
            name="chebyshev",
        )(
            sources.T,
            diag_coef.reshape(blk_rows, size),
            tiles,
            tile_cols,
            send_rows.reshape(4, 1, sent),
            recv_rows,
            bounds,
        )
        result, norm = pl.pallas_call(
            finish,
            out_shape=(
                jax.ShapeDtypeStruct((rows, columns), F32),
                jax.ShapeDtypeStruct((1, columns), F32),
            ),
            in_specs=[pl.BlockSpec(memory_space=vmem)] * 2,
            out_specs=(pl.BlockSpec(memory_space=vmem), pl.BlockSpec(memory_space=vmem)),
            name="finish",
        )(held, norms)
        return result, norm.reshape(columns)

    return jax.shard_map(
        on_device,
        mesh=mesh,
        in_specs=(
            P(),
            P(("patch", "sub")),
            P(("patch", "sub"), None, None, None),
            P(("patch", "sub"), None),
            P(("patch", "sub"), None, None),
            P(("patch", "sub"), None),
            P(),
        ),
        out_specs=(P(("patch", "sub"), None), P()),
        check_vma=False,
    )
```

profile of v0, /device:TPU:0, one launch (start us, length us, event | category | flops | bytes accessed | tf_op | source)
XLA Modules:
  0.0 54.2 jit_solution(15956998085446926968)
XLA Ops:
  0.6 51.9 %chebyshev.1 = (f32[512,128]{1,0:T(8,128)}, f32[32,1,128]{2,1,0:T(1,128)}) custom-call(s32[2,128]{1,0:T(2,128)} %bitcast.6, f32[4,128]{1,0:T(4,128)} %bitcast.4, f32[4,6,128,128]{3,2,1,0:T(8,128)} %tiles_hbm.1, s32[4,6]{1,0:T(4,128)} %cols_ref.1, s32[4,1,128]{2,1,0:T(1,128)} %bitcast.5, s32[1,512]{1,0:T(1,128)} %receives_ref.1, f32[2]{0:T(128)} %bounds_ref.1), custom_call_target="tpu_custom_call" | custom-call | tf_op jit(solution)/shard_map/chebyshev/pallas_call | solution.py:330
  52.5 1.7 %finish.1 = (f32[512,128]{1,0:T(8,128)}, f32[1,128]{1,0:T(1,128)}) custom-call(f32[512,128]{1,0:T(8,128)} %get-tuple-element.6.solution_ref, f32[32,1,128]{2,1,0:T(1,128)} %get-tuple-element.7.norms_ref), custom_call_target="tpu_custom_call" | custom-call | tf_op jit(solution)/shard_map/finish/pallas_call | solution.py:392
where the time goes:
time: 54.4 us; the launch traced here: 54.2 us
  Pallas kernels  53.5 us (98%)
  between operations  0.64 us (1%)
    pallas_call x1, Pallas kernels, on_device(): pl.pallas_call(functools.partial(kernel, n_patch, n_sub), out_shape=(jax....  51.9 us
    pallas_call x1, Pallas kernels, on_device(): pl.pallas_call(finish, out_shape=(jax.ShapeDtypeStruct((rows, columns), F...  1.68 us

commit v1 on v0

v1 whole, which is shorter than its diff:
```python
import functools

import jax
import jax.numpy as jnp
from jax import lax
from jax.experimental import pallas as pl
from jax.experimental.pallas import tpu as pltpu
from jax.sharding import PartitionSpec as P

ITERS = 8
MESH = pl.DeviceIdType.MESH
F32 = jnp.float32
BF16 = jnp.bfloat16


def halves(value):
    high = value.astype(BF16)
    return high, (value - high.astype(F32)).astype(BF16)


def product(high, low, pair, columns):
    wide = jnp.dot(high, pair, preferred_element_type=F32)
    narrow = jnp.dot(low, pair[:, :columns], preferred_element_type=F32)
    return wide[:, :columns] + wide[:, columns:] + narrow


def exact(high, low, counts):
    return jnp.dot(high, counts, preferred_element_type=F32) + jnp.dot(
        low, counts, preferred_element_type=F32
    )


def kernel(
    n_patch, n_sub,
    sources_hbm, diag_hbm, tiles_hbm, cols_hbm, sends_hbm, receives_hbm, bounds_hbm,
    solution_ref, norm_ref,
    sources_ref, diag_ref, cols_ref, sends_ref, receives_ref, bounds_ref,
    tiles_ref, near_hi, near_lo, far_hi, far_lo, halo_hi, halo_lo,
    near_first_hi, near_first_lo, far_first_hi, far_first_lo,
    direction_ref, residual_ref, packed_residual, total_ref, own_total, pair_ref, heard_pair,
    packed_ref, message_ref, heard_ref, heard_rows, heard_counts, norms_ref, counts_ref,
    packed_counts, pick_ref, place_ref, keeps_ref, gains_ref,
    back_hi, back_lo, echo_out, echo_in, echo_hi, echo_lo, echo_ref,
    input_sems, tile_sems, row_send, row_recv, echo_sems,
    send_sems, recv_sems, norm_send, norm_recv,
):
    blk_rows, per_row, size, _ = tiles_hbm.shape
    rows = blk_rows * size
    n_src, columns = sources_ref.shape
    sent = sends_ref.shape[2]
    halo = receives_ref.shape[1]
    packed_rows = 4 * sent
    patch, sub = lax.axis_index("patch"), lax.axis_index("sub")
    devices = n_patch * n_sub
    me = patch * n_sub + sub
    patch_odd, sub_odd = lax.rem(patch, 2), lax.rem(sub, 2)

    partners = [
        (lax.rem(patch + n_patch - 1 + 2 * patch_odd, n_patch), sub),
        (lax.rem(patch + n_patch + 1 - 2 * patch_odd, n_patch), sub),
        (patch, lax.rem(sub + n_sub - 1 + 2 * sub_odd, n_sub)),
        (patch, lax.rem(sub + n_sub + 1 - 2 * sub_odd, n_sub)),
    ]
    sides = [patch_odd, 1 - patch_odd, 2 + sub_odd, 3 - sub_odd]
    spans = [pl.ds(g * sent, sent) for g in range(4)]

    barrier = pltpu.get_barrier_semaphore()
    if n_patch // 2 + n_sub // 2 <= ITERS:
        for partner in partners:
            pl.semaphore_signal(barrier, inc=1, device_id=partner, device_id_type=MESH)
        awaited = 4
    else:
        @pl.loop(1, devices)
        def _(step):
            other = lax.rem(me + step, devices)
            pl.semaphore_signal(
                barrier, inc=1, device_id=(other // n_sub, lax.rem(other, n_sub)), device_id_type=MESH
            )
        awaited = devices - 1

    inputs = [
        pltpu.make_async_copy(source, target, input_sems.at[i])
        for i, (source, target) in enumerate((
            (sends_hbm, sends_ref), (receives_hbm, receives_ref), (sources_hbm, sources_ref),
            (cols_hbm, cols_ref), (diag_hbm, diag_ref), (bounds_hbm, bounds_ref),
        ))
    ]
    for copy in inputs:
        copy.start()
    copies = [
        pltpu.make_async_copy(tiles_hbm.at[b], tiles_ref.at[b], tile_sems.at[b])
        for b in range(blk_rows)
    ]
    for copy in copies:
        copy.start()
    for copy in inputs:
        copy.wait()

    low_end = jnp.full((1, columns), bounds_ref[0], F32)
    high_end = jnp.full((1, columns), bounds_ref[1], F32)
    centre = (low_end + high_end) / 2.0
    half_width = (high_end - low_end) / 2.0
    ratio = centre / half_width
    damping = 1.0 / ratio
    for k in range(ITERS - 1):
        damping_next = 1.0 / (2.0 * ratio - damping)
        keeps_ref[k] = damping_next * damping
        gains_ref[k] = 2.0 * damping_next / half_width
        damping = damping_next

    def counted(ids):
        total = jnp.zeros(ids.shape, F32)
        for s in range(n_src):
            total = total + jnp.where(sources_ref[s : s + 1, :] == ids, 1.0, 0.0)
        return total

    counts_ref[...] = counted(
        me * rows + lax.broadcasted_iota(jnp.int32, (rows, columns), 0)
    ).astype(BF16)

    def as_column(row, width):
        return jnp.broadcast_to(row, (width, row.shape[1])).T

    for g in range(4):
        wide = as_column(sends_ref[sides[g]], rows)
        pick_ref[spans[g]] = jnp.where(
            wide == lax.broadcasted_iota(jnp.int32, (sent, rows), 1), 1.0, 0.0
        ).astype(BF16)
    for i in range(halo // size):
        wide = as_column(receives_ref[:, i * size : (i + 1) * size], sent)
        for g in range(4):
            place_ref[pl.ds(i * size, size), spans[g]] = jnp.where(
                wide == sides[g] * sent + lax.broadcasted_iota(jnp.int32, (size, sent), 1), 1.0, 0.0
            ).astype(BF16)

    eye = lax.broadcasted_iota(jnp.int32, (size, size), 0) == lax.broadcasted_iota(
        jnp.int32, (size, size), 1
    )
    for b in range(blk_rows):
        copies[b].wait()
        for c in range(blk_rows + halo // size):
            block = jnp.zeros((size, size), F32)
            for n in range(per_row):
                block = block + tiles_ref[b, n] * (cols_ref[b, n] == c).astype(F32)
            if c == b:
                block = block + jnp.where(eye, diag_ref[b : b + 1, :], 0.0)
            high, low = halves(block)
            at = pl.ds(b * size, size)
            if c < blk_rows:
                near_hi[at, pl.ds(c * size, size)] = high
                near_lo[at, pl.ds(c * size, size)] = low
            else:
                place_at = pl.ds((c - blk_rows) * size, size)
                halo_hi[at, place_at] = high
                halo_lo[at, place_at] = low

    pl.semaphore_wait(barrier, awaited)

    def row_copy(g):
        return pltpu.make_async_remote_copy(
            src_ref=sends_ref.at[sides[g]], dst_ref=heard_rows.at[g],
            send_sem=row_send.at[g], recv_sem=row_recv.at[g],
            device_id=partners[g], device_id_type=MESH,
        )

    for g in range(4):
        row_copy(g).start()

    def chosen(matrix):
        return jnp.dot(pick_ref[...], matrix[...], preferred_element_type=F32).astype(BF16)

    for halo_part, far in ((halo_hi, far_hi), (halo_lo, far_lo)):
        far[...] = jnp.dot(
            halo_part[...], place_ref[...], preferred_element_type=F32
        ).astype(BF16)
    far_first_hi[...] = chosen(far_hi)
    far_first_lo[...] = chosen(far_lo)

    first, others = spans[0], pl.ds(sent, 3 * sent)
    back_hi[...] = far_first_hi[first, first]
    back_lo[...] = far_first_lo[first, first]
    echo_out[...] = back_hi[...].astype(F32) + back_lo[...].astype(F32)
    echo_copy = pltpu.make_async_remote_copy(
        src_ref=echo_out, dst_ref=echo_in, send_sem=echo_sems.at[0], recv_sem=echo_sems.at[1],
        device_id=partners[0], device_id_type=MESH,
    )
    echo_copy.start()
    near_first_hi[...] = chosen(near_hi)
    near_first_lo[...] = chosen(near_lo)
    packed_counts[...] = jnp.dot(pick_ref[...], counts_ref[...], preferred_element_type=F32)
    total_ref[...] = exact(near_first_hi[...], near_first_lo[...], counts_ref[...])

    def hear_counts(g):
        row_copy(g).wait_recv()
        base = (partners[g][0] * n_sub + partners[g][1]) * rows
        heard_counts[spans[g]] = counted(base + as_column(heard_rows[g], columns)).astype(BF16)

    def mail(source, slot, g):
        return pltpu.make_async_remote_copy(
            src_ref=source, dst_ref=heard_ref.at[slot, g],
            send_sem=send_sems.at[slot, g], recv_sem=recv_sems.at[slot, g],
            device_id=partners[g], device_id_type=MESH,
        )

    def hear(slot, g):
        mail(packed_ref.at[slot, g], slot, g).wait_recv()
        value = heard_ref[slot, g]
        if g == 0:
            value = value - echo_ref[...]
        high, low = halves(value)
        heard_pair[spans[g], :columns] = high
        heard_pair[spans[g], columns:] = low

    for g in (3, 2, 1, 0):
        hear_counts(g)
    keep, gain = keeps_ref[0], gains_ref[0]
    total = total_ref[...] + exact(far_first_hi[...], far_first_lo[...], heard_counts[...])
    rest = packed_counts[...] - total / centre
    packed_residual[...] = rest
    fresh = keep * (packed_counts[...] / centre) + gain * rest
    for g in range(4):
        packed_ref[1, g] = fresh[g * sent : (g + 1) * sent]
    for g in range(4):
        mail(packed_ref.at[1, g], 1, g).start()

    def send_direction(direction):
        direction_ref[...] = direction
        high, low = halves(direction)
        pair_ref[:, :columns] = high
        pair_ref[:, columns:] = low

    right_side = counts_ref[...].astype(F32)
    total = exact(near_hi[...], near_lo[...], counts_ref[...]) + exact(
        far_hi[...], far_lo[...], heard_counts[...]
    )
    residual = right_side - total / centre
    residual_ref[...] = residual
    before = right_side / centre
    direction = keep * before + gain * residual
    solution_ref[...] = before + direction
    send_direction(direction)

    far_first_hi[first, first] = jnp.zeros((sent, sent), BF16)
    far_first_lo[first, first] = jnp.zeros((sent, sent), BF16)
    echo_ref[...] = jnp.zeros((sent, columns), F32)
    echo_copy.wait()
    echo_hi[...], echo_lo[...] = halves(echo_in[...])

    def far_product(at, part):
        return product(far_first_hi[at, part], far_first_lo[at, part], heard_pair[part], columns)

    def step(slot):
        keep, gain = keeps_ref[slot], gains_ref[slot]
        total_ref[...] = product(near_first_hi[...], near_first_lo[...], pair_ref[...], columns)
        hear(slot, 3)
        everything, middle = pl.ds(0, packed_rows), pl.ds(sent, 2 * sent)
        total_ref[...] = total_ref[...] + far_product(everything, spans[3])
        hear(slot, 2)
        hear(slot, 1)
        rest = packed_residual[first] - (total_ref[first] + far_product(first, middle))
        packed_residual[first] = rest
        message_ref[slot + 1] = keep * packed_ref[slot, 0] + gain * rest
        mail(message_ref.at[slot + 1], slot + 1, 0).start()
        total_ref[others] = total_ref[others] + far_product(others, middle)
        hear(slot, 0)
        rest = packed_residual[others] - (total_ref[others] + far_product(others, first))
        packed_residual[others] = rest
        for g in (1, 2, 3):
            packed_ref[slot + 1, g] = (
                keep * packed_ref[slot, g] + gain * rest[(g - 1) * sent : g * sent]
            )
        for g in (1, 2, 3):
            mail(packed_ref.at[slot + 1, g], slot + 1, g).start()

        residual = residual_ref[...] - (
            product(near_hi[...], near_lo[...], pair_ref[...], columns)
            + product(far_hi[...], far_lo[...], heard_pair[...], columns)
        )
        residual_ref[...] = residual
        direction = keep * direction_ref[...] + gain * residual
        solution_ref[...] = solution_ref[...] + direction
        send_direction(direction)
        rest = packed_residual[first] - product(back_hi[...], back_lo[...], heard_pair[first], columns)
        packed_residual[first] = rest
        packed_ref[slot + 1, 0] = keep * packed_ref[slot, 0] + gain * rest
        high, low = halves(packed_ref[slot, 0])
        echo_ref[...] = gain * product(
            echo_hi[...], echo_lo[...], jnp.concatenate([high, low], axis=1), columns
        )

    lax.fori_loop(1, ITERS - 1, lambda slot, _: (step(slot), 0)[1], 0)

    slot = ITERS - 1
    total = product(near_hi[...], near_lo[...], pair_ref[...], columns)
    own_total[...] = residual_ref[...] - total
    for groups in ((3,), (2,), (1, 0)):
        for g in groups:
            hear(slot, g)
        part = pl.ds(groups[-1] * sent, len(groups) * sent)
        total = product(far_hi[:, part], far_lo[:, part], heard_pair[part], columns)
        if groups[-1]:
            own_total[...] = own_total[...] - total
    final = own_total[...] - total
    norms_ref[me] = jnp.sum(final * final, axis=0, keepdims=True)

    @pl.loop(1, devices)
    def _(step):
        other = lax.rem(me + step, devices)
        pltpu.make_async_remote_copy(
            src_ref=norms_ref.at[me], dst_ref=norms_ref.at[me],
            send_sem=norm_send, recv_sem=norm_recv,
            device_id=(other // n_sub, lax.rem(other, n_sub)), device_id_type=MESH,
        ).start()

    for g in range(4):
        row_copy(g).wait_send()
        for slot in range(1, ITERS):
            mail(packed_ref.at[slot, g], slot, g).wait_send()
    parts = norms_ref.at[pl.ds(0, devices - 1)]
    pltpu.make_async_copy(parts, parts, norm_recv).wait()
    pltpu.make_async_copy(parts, parts, norm_send).wait()
    norm_ref[...] = jnp.sqrt(jnp.sum(norms_ref[...], axis=0))


def finish(held_ref, norm_ref, result_hbm, root_hbm, sems):
    copies = [
        pltpu.make_async_copy(held_ref, result_hbm, sems.at[0]),
        pltpu.make_async_copy(norm_ref, root_hbm, sems.at[1]),
    ]
    for copy in copies:
        copy.start()
    for copy in copies:
        copy.wait()


def solution(mesh):
    n_patch, n_sub = mesh.shape["patch"], mesh.shape["sub"]

    def on_device(sources, diag_coef, tiles, tile_cols, send_rows, recv_rows, bounds):
        blk_rows, per_row, size, _ = tiles.shape
        rows = diag_coef.shape[0]
        columns = sources.shape[0]
        n_src = sources.shape[1]
        sent = send_rows.shape[2]
        halo = recv_rows.shape[1]
        packed = 4 * sent
        vmem, smem = pltpu.VMEM, pltpu.SMEM
        dma = pltpu.SemaphoreType.DMA
        anywhere = pl.BlockSpec(memory_space=pl.ANY)
        held, norm = pl.pallas_call(
            functools.partial(kernel, n_patch, n_sub),
            out_shape=(vmem((rows, columns), F32), vmem((1, columns), F32)),
            in_specs=[anywhere] * 7,
            out_specs=(pl.BlockSpec(memory_space=vmem), pl.BlockSpec(memory_space=vmem)),
            scratch_shapes=[
                vmem((n_src, columns), jnp.int32),
                vmem((blk_rows, size), F32),
                smem((blk_rows, per_row), jnp.int32),
                vmem((4, 1, sent), jnp.int32),
                vmem((1, halo), jnp.int32),
                smem((2,), F32),
                vmem(tiles.shape, F32),
                vmem((rows, rows), BF16),
                vmem((rows, rows), BF16),
                vmem((rows, packed), BF16),
                vmem((rows, packed), BF16),
                vmem((rows, halo), BF16),
                vmem((rows, halo), BF16),
                vmem((packed, rows), BF16),
                vmem((packed, rows), BF16),
                vmem((packed, packed), BF16),
                vmem((packed, packed), BF16),
                vmem((rows, columns), F32),
                vmem((rows, columns), F32),
                vmem((packed, columns), F32),
                vmem((packed, columns), F32),
                vmem((rows, columns), F32),
                vmem((rows, 2 * columns), BF16),
                vmem((packed, 2 * columns), BF16),
                vmem((ITERS, 4, sent, columns), F32),
                vmem((ITERS, sent, columns), F32),
                vmem((ITERS, 4, sent, columns), F32),
                vmem((4, 1, sent), jnp.int32),
                vmem((packed, columns), BF16),
                vmem((n_patch * n_sub, 1, columns), F32),
                vmem((rows, columns), BF16),
                vmem((packed, columns), F32),
                vmem((packed, rows), BF16),
                vmem((halo, packed), BF16),
                vmem((ITERS, 1, columns), F32),
                vmem((ITERS, 1, columns), F32),
                vmem((sent, sent), BF16),
                vmem((sent, sent), BF16),
                vmem((sent, sent), F32),
                vmem((sent, sent), F32),
                vmem((sent, sent), BF16),
                vmem((sent, sent), BF16),
                vmem((sent, columns), F32),
                dma((6,)),
                dma((blk_rows,)),
                dma((4,)),
                dma((4,)),
                dma((2,)),
                dma((ITERS, 4)),
                dma((ITERS, 4)),
                dma,
                dma,
            ],
            compiler_params=pltpu.CompilerParams(collective_id=0, has_side_effects=True),
            name="chebyshev",
        )(
            sources.T,
            diag_coef.reshape(blk_rows, size),
            tiles,
            tile_cols,
            send_rows.reshape(4, 1, sent),
            recv_rows,
            bounds,
        )
        result, root = pl.pallas_call(
            finish,
            out_shape=(
                jax.ShapeDtypeStruct((rows, columns), F32),
                jax.ShapeDtypeStruct((1, columns), F32),
            ),
            in_specs=[pl.BlockSpec(memory_space=vmem)] * 2,
            out_specs=(anywhere, anywhere),
            scratch_shapes=[dma((2,))],
            name="finish",
        )(pltpu.with_memory_space_constraint(held, vmem), pltpu.with_memory_space_constraint(norm, vmem))
        return result, root.reshape(columns)

    return jax.shard_map(
        on_device,
        mesh=mesh,
        in_specs=(
            P(),
            P(("patch", "sub")),
            P(("patch", "sub"), None, None, None),
            P(("patch", "sub"), None),
            P(("patch", "sub"), None, None),
            P(("patch", "sub"), None),
            P(),
        ),
        out_specs=(P(("patch", "sub"), None), P()),
        check_vma=False,
    )
```

time: 54.4 us -> 51.1 us (0.939)
  Pallas kernels: 53.5 us -> 50.2 us
    pallas_call x1, Pallas kernels: 51.9 us -> 49.5 us  [on_device(): pl.pallas_call(functools.partial(kernel, n_patch, n_sub), out_shape=(vmem...]
    pallas_call x1, Pallas kernels: 1.68 us -> 0.72 us  [on_device(): pl.pallas_call(finish, out_shape=(jax.ShapeDtypeStruct((rows, columns), F...]
where the time goes in v1:
time: 51.1 us; the launch traced here: 50.9 us
  Pallas kernels  50.2 us (98%)
  between operations  0.64 us (1%)
    pallas_call x1, Pallas kernels, on_device(): pl.pallas_call(functools.partial(kernel, n_patch, n_sub), out_shape=(vmem...  49.5 us

profile of v1, /device:TPU:0, one launch (start us, length us, event | category | flops | bytes accessed | tf_op | source)
XLA Modules:
  0.0 50.9 jit_solution(110618604609879762)
XLA Ops:
  0.6 49.5 %chebyshev.1 = (f32[512,128]{1,0:T(8,128)S(1)}, f32[1,128]{1,0:T(1,128)S(1)}) custom-call(s32[2,128]{1,0:T(2,128)} %bitcast.6, f32[4,128]{1,0:T(4,128)} %bitcast.4, f32[4,6,128,128]{3,2,1,0:T(8,128)} %tiles_hbm.1, s32[4,6]{1,0:T(4,128)} %cols_hbm.1, s32[4,1,128]{2,1,0:T(1,128)} %bitcast.5, s32[1,512]{1,0:T(1,128)} %receives_hbm.1, f32[2]{0:T(128)} %bounds_hbm.1), custom_call_target="tpu_custom_call" | custom-call | tf_op jit(solution)/shard_map/chebyshev/pallas_call | solution.py:350
  50.2 0.7 %finish.1 = (f32[512,128]{1,0:T(8,128)}, f32[1,128]{1,0:T(1,128)}) custom-call(f32[512,128]{1,0:T(8,128)S(1)} %get-tuple-element.6.held_ref, f32[1,128]{1,0:T(1,128)S(1)} %get-tuple-element.7.norm_ref), custom_call_target="tpu_custom_call" | custom-call | tf_op jit(solution)/shard_map/finish/pallas_call | solution.py:420

commit v2 on v1

--- a/solution.py
+++ b/solution.py
@@ -18,10 +18,35 @@
     return high, (value - high.astype(F32)).astype(BF16)
 
 
-def product(high, low, pair, columns):
+def product(high, low, mixed_pair):
+    return jnp.dot(high, mixed_pair, preferred_element_type=F32) + jnp.dot(
+        low, mixed_pair, preferred_element_type=F32
+    )
+
+
+def whole(high, low, pair):
+    columns = pair.shape[1] // 2
     wide = jnp.dot(high, pair, preferred_element_type=F32)
     narrow = jnp.dot(low, pair[:, :columns], preferred_element_type=F32)
     return wide[:, :columns] + wide[:, columns:] + narrow
+
+
+def turn(value):
+    return pltpu.roll(value, value.shape[1] // 2, 1)
+
+
+def in_left(value):
+    lanes = lax.broadcasted_iota(jnp.int32, value.shape, 1)
+    return lanes < value.shape[1] // 2
+
+
+def doubled(value):
+    other, left = turn(value), in_left(value)
+    return jnp.where(left, value, other), jnp.where(left, other, value)
+
+
+def fold(wide):
+    return wide + turn(wide)
 
 
 def exact(high, low, counts):
@@ -37,8 +62,8 @@
     sources_ref, diag_ref, cols_ref, sends_ref, receives_ref, bounds_ref,
     tiles_ref, near_hi, near_lo, far_hi, far_lo, halo_hi, halo_lo,
     near_first_hi, near_first_lo, far_first_hi, far_first_lo,
-    direction_ref, residual_ref, packed_residual, total_ref, own_total, pair_ref, heard_pair,
-    packed_ref, message_ref, heard_ref, heard_rows, heard_counts, norms_ref, counts_ref,
+    direction_ref, residual_ref, packed_residual, packed_direction, total_ref, totals_ref, own_total, pair_ref, heard_pair, heard_mixed,
+    outbox_ref, heard_ref, heard_rows, heard_counts, norms_ref, counts_ref,
     packed_counts, pick_ref, place_ref, keeps_ref, gains_ref,
     back_hi, back_lo, echo_out, echo_in, echo_hi, echo_lo, echo_ref,
     input_sems, tile_sems, row_send, row_recv, echo_sems,
@@ -185,43 +210,67 @@
         device_id=partners[0], device_id_type=MESH,
     )
     echo_copy.start()
-    near_first_hi[...] = chosen(near_hi)
-    near_first_lo[...] = chosen(near_lo)
-    packed_counts[...] = jnp.dot(pick_ref[...], counts_ref[...], preferred_element_type=F32)
-    total_ref[...] = exact(near_first_hi[...], near_first_lo[...], counts_ref[...])
+    own_total[...] = exact(near_hi[...], near_lo[...], counts_ref[...])
+    high, low = halves(own_total[...])
+    taken = jnp.dot(
+        pick_ref[...], jnp.concatenate([counts_ref[...], high, low], axis=1), preferred_element_type=F32
+    )
+    packed_counts[...] = taken[:, :columns]
+    total_ref[...] = taken[:, columns : 2 * columns] + taken[:, 2 * columns :]
 
     def hear_counts(g):
         row_copy(g).wait_recv()
         base = (partners[g][0] * n_sub + partners[g][1]) * rows
         heard_counts[spans[g]] = counted(base + as_column(heard_rows[g], columns)).astype(BF16)
 
-    def mail(source, slot, g):
+    part = sent // 2
+
+    def mail(slot, h, g):
         return pltpu.make_async_remote_copy(
-            src_ref=source, dst_ref=heard_ref.at[slot, g],
-            send_sem=send_sems.at[slot, g], recv_sem=recv_sems.at[slot, g],
+            src_ref=outbox_ref.at[slot, h, g], dst_ref=heard_ref.at[slot, h, g],
+            send_sem=send_sems.at[slot, h, g], recv_sem=recv_sems.at[slot, h, g],
             device_id=partners[g], device_id_type=MESH,
         )
 
-    def hear(slot, g):
-        mail(packed_ref.at[slot, g], slot, g).wait_recv()
-        value = heard_ref[slot, g]
-        if g == 0:
-            value = value - echo_ref[...]
-        high, low = halves(value)
-        heard_pair[spans[g], :columns] = high
-        heard_pair[spans[g], columns:] = low
+    def post(slot, h, groups, fresh):
+        for i, g in enumerate(groups):
+            top, bottom = fresh[i * sent : i * sent + part], fresh[i * sent + part : (i + 1) * sent]
+            outbox_ref[slot, h, g] = jnp.where(in_left(top), top, bottom)
+        for g in groups:
+            mail(slot, h, g).start()
+
+    half = columns // 2
+    sides_of = [slice(0, half), slice(half, columns)]
+
+    def hear(slot, h, groups):
+        for g in groups:
+            mail(slot, h, g).wait_recv()
+        for g in groups:
+            for i, twice in enumerate(doubled(heard_ref[slot, h, g])):
+                at = pl.ds(g * sent + i * part, part)
+                if g == 0:
+                    twice = twice - echo_ref[h, pl.ds(i * part, part)]
+                high = twice.astype(BF16)
+                rounded = high.astype(F32)
+                below = twice - rounded
+                heard_mixed[h, at] = jnp.where(in_left(twice), rounded, below).astype(BF16)
+                low = below.astype(BF16)
+                kept = sides_of[h]
+                heard_pair[at, h * half : (h + 1) * half] = high[:, kept]
+                heard_pair[at, columns + h * half : columns + (h + 1) * half] = low[:, kept]
 
     for g in (3, 2, 1, 0):
         hear_counts(g)
     keep, gain = keeps_ref[0], gains_ref[0]
     total = total_ref[...] + exact(far_first_hi[...], far_first_lo[...], heard_counts[...])
     rest = packed_counts[...] - total / centre
-    packed_residual[...] = rest
-    fresh = keep * (packed_counts[...] / centre) + gain * rest
-    for g in range(4):
-        packed_ref[1, g] = fresh[g * sent : (g + 1) * sent]
-    for g in range(4):
-        mail(packed_ref.at[1, g], 1, g).start()
+    residuals, directions = doubled(rest), doubled(
+        keep * (packed_counts[...] / centre) + gain * rest
+    )
+    for h in range(2):
+        packed_residual[h] = residuals[h]
+        packed_direction[h] = directions[h]
+        post(1, h, range(4), directions[h])
 
     def send_direction(direction):
         direction_ref[...] = direction
@@ -230,9 +279,7 @@
         pair_ref[:, columns:] = low
 
     right_side = counts_ref[...].astype(F32)
-    total = exact(near_hi[...], near_lo[...], counts_ref[...]) + exact(
-        far_hi[...], far_lo[...], heard_counts[...]
-    )
+    total = own_total[...] + exact(far_hi[...], far_lo[...], heard_counts[...])
     residual = right_side - total / centre
     residual_ref[...] = residual
     before = right_side / centre
@@ -240,64 +287,76 @@
     solution_ref[...] = before + direction
     send_direction(direction)
 
+    near_first_hi[...] = chosen(near_hi)
+    near_first_lo[...] = chosen(near_lo)
     far_first_hi[first, first] = jnp.zeros((sent, sent), BF16)
     far_first_lo[first, first] = jnp.zeros((sent, sent), BF16)
-    echo_ref[...] = jnp.zeros((sent, columns), F32)
+    echo_ref[...] = jnp.zeros((2, sent, columns), F32)
     echo_copy.wait()
     echo_hi[...], echo_lo[...] = halves(echo_in[...])
 
-    def far_product(at, part):
-        return product(far_first_hi[at, part], far_first_lo[at, part], heard_pair[part], columns)
+    def start_totals():
+        totals = doubled(whole(near_first_hi[...], near_first_lo[...], pair_ref[...]))
+        for h in range(2):
+            totals_ref[h] = packed_residual[h] - totals[h]
+
+    def far_product(at, span, h):
+        return fold(product(far_first_hi[at, span], far_first_lo[at, span], heard_mixed[h, span]))
+
+    start_totals()
+    everything = pl.ds(0, packed_rows)
 
     def step(slot):
         keep, gain = keeps_ref[slot], gains_ref[slot]
-        total_ref[...] = product(near_first_hi[...], near_first_lo[...], pair_ref[...], columns)
-        hear(slot, 3)
-        everything, middle = pl.ds(0, packed_rows), pl.ds(sent, 2 * sent)
-        total_ref[...] = total_ref[...] + far_product(everything, spans[3])
-        hear(slot, 2)
-        hear(slot, 1)
-        rest = packed_residual[first] - (total_ref[first] + far_product(first, middle))
-        packed_residual[first] = rest
-        message_ref[slot + 1] = keep * packed_ref[slot, 0] + gain * rest
-        mail(message_ref.at[slot + 1], slot + 1, 0).start()
-        total_ref[others] = total_ref[others] + far_product(others, middle)
-        hear(slot, 0)
-        rest = packed_residual[others] - (total_ref[others] + far_product(others, first))
-        packed_residual[others] = rest
-        for g in (1, 2, 3):
-            packed_ref[slot + 1, g] = (
-                keep * packed_ref[slot, g] + gain * rest[(g - 1) * sent : g * sent]
-            )
-        for g in (1, 2, 3):
-            mail(packed_ref.at[slot + 1, g], slot + 1, g).start()
+        for h in range(2):
+            hear(slot, h, (3, 2, 1))
+            two = pl.ds(0, 2 * sent)
+            rest = totals_ref[h, two] - far_product(two, others, h)
+            packed_residual[h, two] = rest
+            rest = rest[:sent]
+            post(slot + 1, h, (0,), keep * packed_direction[h, first] + gain * rest)
+            hear(slot, h, (0,))
+            for g in (1, 2, 3):
+                at = spans[g]
+                if g == 1:
+                    rest = packed_residual[h, at] - far_product(at, first, h)
+                else:
+                    rest = totals_ref[h, at] - far_product(at, everything, h)
+                packed_residual[h, at] = rest
+                fresh = keep * packed_direction[h, at] + gain * rest
+                packed_direction[h, at] = fresh
+                post(slot + 1, h, (g,), fresh)
 
         residual = residual_ref[...] - (
-            product(near_hi[...], near_lo[...], pair_ref[...], columns)
-            + product(far_hi[...], far_lo[...], heard_pair[...], columns)
+            whole(near_hi[...], near_lo[...], pair_ref[...])
+            + whole(far_hi[...], far_lo[...], heard_pair[...])
         )
         residual_ref[...] = residual
         direction = keep * direction_ref[...] + gain * residual
         solution_ref[...] = solution_ref[...] + direction
         send_direction(direction)
-        rest = packed_residual[first] - product(back_hi[...], back_lo[...], heard_pair[first], columns)
-        packed_residual[first] = rest
-        packed_ref[slot + 1, 0] = keep * packed_ref[slot, 0] + gain * rest
-        high, low = halves(packed_ref[slot, 0])
-        echo_ref[...] = gain * product(
-            echo_hi[...], echo_lo[...], jnp.concatenate([high, low], axis=1), columns
+        back = doubled(whole(back_hi[...], back_lo[...], heard_pair[first]))
+        before = [packed_direction[h, first] for h in range(2)]
+        high, low = halves(jnp.where(in_left(before[0]), *before))
+        echo = doubled(
+            gain * whole(echo_hi[...], echo_lo[...], jnp.concatenate([high, low], axis=1))
         )
+        for h in range(2):
+            echo_ref[h] = echo[h]
+            rest = packed_residual[h, first] - back[h]
+            packed_residual[h, first] = rest
+            packed_direction[h, first] = keep * before[h] + gain * rest
+        start_totals()
 
     lax.fori_loop(1, ITERS - 1, lambda slot, _: (step(slot), 0)[1], 0)
 
     slot = ITERS - 1
-    total = product(near_hi[...], near_lo[...], pair_ref[...], columns)
-    own_total[...] = residual_ref[...] - total
-    for groups in ((3,), (2,), (1, 0)):
-        for g in groups:
-            hear(slot, g)
-        part = pl.ds(groups[-1] * sent, len(groups) * sent)
-        total = product(far_hi[:, part], far_lo[:, part], heard_pair[part], columns)
+    own_total[...] = residual_ref[...] - whole(near_hi[...], near_lo[...], pair_ref[...])
+    hear(slot, 0, (3, 2, 1, 0))
+    for groups in ((3, 2), (1, 0)):
+        hear(slot, 1, groups)
+        span = pl.ds(groups[-1] * sent, len(groups) * sent)
+        total = whole(far_hi[:, span], far_lo[:, span], heard_pair[span])
         if groups[-1]:
             own_total[...] = own_total[...] - total
     final = own_total[...] - total
@@ -315,7 +374,8 @@
     for g in range(4):
         row_copy(g).wait_send()
         for slot in range(1, ITERS):
-            mail(packed_ref.at[slot, g], slot, g).wait_send()
+            for h in range(2):
+                mail(slot, h, g).wait_send()
     parts = norms_ref.at[pl.ds(0, devices - 1)]
     pltpu.make_async_copy(parts, parts, norm_recv).wait()
     pltpu.make_async_copy(parts, parts, norm_send).wait()
@@ -372,14 +432,16 @@
                 vmem((packed, packed), BF16),
                 vmem((rows, columns), F32),
                 vmem((rows, columns), F32),
+                vmem((2, packed, columns), F32),
+                vmem((2, packed, columns), F32),
                 vmem((packed, columns), F32),
-                vmem((packed, columns), F32),
+                vmem((2, packed, columns), F32),
                 vmem((rows, columns), F32),
                 vmem((rows, 2 * columns), BF16),
                 vmem((packed, 2 * columns), BF16),
-                vmem((ITERS, 4, sent, columns), F32),
-                vmem((ITERS, sent, columns), F32),
-                vmem((ITERS, 4, sent, columns), F32),
+                vmem((2, packed, columns), BF16),
+                vmem((ITERS, 2, 4, sent // 2, columns), F32),
+                vmem((ITERS, 2, 4, sent // 2, columns), F32),
                 vmem((4, 1, sent), jnp.int32),
                 vmem((packed, columns), BF16),
                 vmem((n_patch * n_sub, 1, columns), F32),
@@ -395,14 +457,14 @@
                 vmem((sent, sent), F32),
                 vmem((sent, sent), BF16),
                 vmem((sent, sent), BF16),
-                vmem((sent, columns), F32),
+                vmem((2, sent, columns), F32),
                 dma((6,)),
                 dma((blk_rows,)),
                 dma((4,)),
                 dma((4,)),
                 dma((2,)),
-                dma((ITERS, 4)),
-                dma((ITERS, 4)),
+                dma((ITERS, 2, 4)),
+                dma((ITERS, 2, 4)),
                 dma,
                 dma,
             ],

time: 51.1 us -> 49.7 us (0.973)
  Pallas kernels: 50.2 us -> 48.8 us
    pallas_call x1, Pallas kernels: 49.5 us -> 48.1 us  [on_device(): pl.pallas_call(functools.partial(kernel, n_patch, n_sub), out_shape=(vmem...]
where the time goes in v2:
time: 49.7 us; the launch traced here: 49.5 us
  Pallas kernels  48.8 us (98%)
  between operations  0.64 us (1%)
    pallas_call x1, Pallas kernels, on_device(): pl.pallas_call(functools.partial(kernel, n_patch, n_sub), out_shape=(vmem...  48.1 us

profile of v2, /device:TPU:0, one launch (start us, length us, event | category | flops | bytes accessed | tf_op | source)
XLA Modules:
  0.0 49.5 jit_solution(18267944581033716360)
XLA Ops:
  0.6 48.1 %chebyshev.1 = (f32[512,128]{1,0:T(8,128)S(1)}, f32[1,128]{1,0:T(1,128)S(1)}) custom-call(s32[2,128]{1,0:T(2,128)} %bitcast.6, f32[4,128]{1,0:T(4,128)} %bitcast.4, f32[4,6,128,128]{3,2,1,0:T(8,128)} %tiles_hbm.1, s32[4,6]{1,0:T(4,128)} %cols_hbm.1, s32[4,1,128]{2,1,0:T(1,128)} %bitcast.5, s32[1,512]{1,0:T(1,128)} %receives_hbm.1, f32[2]{0:T(128)} %bounds_hbm.1), custom_call_target="tpu_custom_call" | custom-call | tf_op jit(solution)/shard_map/chebyshev/pallas_call | solution.py:410
  48.8 0.7 %finish.1 = (f32[512,128]{1,0:T(8,128)}, f32[1,128]{1,0:T(1,128)}) custom-call(f32[512,128]{1,0:T(8,128)S(1)} %get-tuple-element.6.held_ref, f32[1,128]{1,0:T(1,128)S(1)} %get-tuple-element.7.norm_ref), custom_call_target="tpu_custom_call" | custom-call | tf_op jit(solution)/shard_map/finish/pallas_call | solution.py:482

commit v3 on v2

--- a/solution.py
+++ b/solution.py
@@ -66,7 +66,7 @@
     outbox_ref, heard_ref, heard_rows, heard_counts, norms_ref, counts_ref,
     packed_counts, pick_ref, place_ref, keeps_ref, gains_ref,
     back_hi, back_lo, echo_out, echo_in, echo_hi, echo_lo, echo_ref,
-    input_sems, tile_sems, row_send, row_recv, echo_sems,
+    input_sems, tile_sems, echo_sems,
     send_sems, recv_sems, norm_send, norm_recv,
 ):
     blk_rows, per_row, size, _ = tiles_hbm.shape
@@ -181,10 +181,15 @@
 
     pl.semaphore_wait(barrier, awaited)
 
+    def arrival(slot, h, g):
+        if g == 0:
+            return recv_sems.at[2 * lax.rem(slot, 4) + h]
+        return recv_sems.at[8 + 3 * (2 * lax.rem(slot, 2) + h) + g - 1]
+
     def row_copy(g):
         return pltpu.make_async_remote_copy(
             src_ref=sends_ref.at[sides[g]], dst_ref=heard_rows.at[g],
-            send_sem=row_send.at[g], recv_sem=row_recv.at[g],
+            send_sem=send_sems.at[0, g], recv_sem=arrival(0, 0, g),
             device_id=partners[g], device_id_type=MESH,
         )
 
@@ -228,15 +233,19 @@
     def mail(slot, h, g):
         return pltpu.make_async_remote_copy(
             src_ref=outbox_ref.at[slot, h, g], dst_ref=heard_ref.at[slot, h, g],
-            send_sem=send_sems.at[slot, h, g], recv_sem=recv_sems.at[slot, h, g],
+            send_sem=send_sems.at[h, g], recv_sem=arrival(slot, h, g),
             device_id=partners[g], device_id_type=MESH,
         )
 
-    def post(slot, h, groups, fresh):
+    def post(slot, h, groups, fresh, begins=False):
         for i, g in enumerate(groups):
             top, bottom = fresh[i * sent : i * sent + part], fresh[i * sent + part : (i + 1) * sent]
             outbox_ref[slot, h, g] = jnp.where(in_left(top), top, bottom)
         for g in groups:
+            if not begins:
+                mail(slot - 1, h, g).wait_send()
+            elif h == 0:
+                row_copy(g).wait_send()
             mail(slot, h, g).start()
 
     half = columns // 2
@@ -270,7 +279,7 @@
     for h in range(2):
         packed_residual[h] = residuals[h]
         packed_direction[h] = directions[h]
-        post(1, h, range(4), directions[h])
+        post(1, h, range(4), directions[h], True)
 
     def send_direction(direction):
         direction_ref[...] = direction
@@ -372,10 +381,8 @@
         ).start()
 
     for g in range(4):
-        row_copy(g).wait_send()
-        for slot in range(1, ITERS):
-            for h in range(2):
-                mail(slot, h, g).wait_send()
+        for h in range(2):
+            mail(ITERS - 1, h, g).wait_send()
     parts = norms_ref.at[pl.ds(0, devices - 1)]
     pltpu.make_async_copy(parts, parts, norm_recv).wait()
     pltpu.make_async_copy(parts, parts, norm_send).wait()
@@ -460,11 +467,9 @@
                 vmem((2, sent, columns), F32),
                 dma((6,)),
                 dma((blk_rows,)),
-                dma((4,)),
-                dma((4,)),
                 dma((2,)),
-                dma((ITERS, 2, 4)),
-                dma((ITERS, 2, 4)),
+                dma((2, 4)),
+                dma((20,)),
                 dma,
                 dma,
             ],

time: 49.7 us -> 48.7 us (0.980)
  Pallas kernels: 48.8 us -> 47.9 us
    pallas_call x1, Pallas kernels: 48.1 us -> 47.2 us  [on_device(): pl.pallas_call(functools.partial(kernel, n_patch, n_sub), out_shape=(vmem...]
where the time goes in v3:
time: 48.7 us; the launch traced here: 48.6 us
  Pallas kernels  47.9 us (98%)
  between operations  0.64 us (1%)
    pallas_call x1, Pallas kernels, on_device(): pl.pallas_call(functools.partial(kernel, n_patch, n_sub), out_shape=(vmem...  47.2 us

profile of v3, /device:TPU:0, one launch (start us, length us, event | category | flops | bytes accessed | tf_op | source)
XLA Modules:
  0.0 48.6 jit_solution(12206449263315083600)
XLA Ops:
  0.6 47.2 %chebyshev.1 = (f32[512,128]{1,0:T(8,128)S(1)}, f32[1,128]{1,0:T(1,128)S(1)}) custom-call(s32[2,128]{1,0:T(2,128)} %bitcast.6, f32[4,128]{1,0:T(4,128)} %bitcast.4, f32[4,6,128,128]{3,2,1,0:T(8,128)} %tiles_hbm.1, s32[4,6]{1,0:T(4,128)} %cols_hbm.1, s32[4,1,128]{2,1,0:T(1,128)} %bitcast.5, s32[1,512]{1,0:T(1,128)} %receives_hbm.1, f32[2]{0:T(128)} %bounds_hbm.1), custom_call_target="tpu_custom_call" | custom-call | tf_op jit(solution)/shard_map/chebyshev/pallas_call | solution.py:417
  47.8 0.7 %finish.1 = (f32[512,128]{1,0:T(8,128)}, f32[1,128]{1,0:T(1,128)}) custom-call(f32[512,128]{1,0:T(8,128)S(1)} %get-tuple-element.6.held_ref, f32[1,128]{1,0:T(1,128)S(1)} %get-tuple-element.7.norm_ref), custom_call_target="tpu_custom_call" | custom-call | tf_op jit(solution)/shard_map/finish/pallas_call | solution.py:487

commit v4 on v3

--- a/solution.py
+++ b/solution.py
@@ -118,9 +118,36 @@
     ]
     for copy in copies:
         copy.start()
-    for copy in inputs:
+    def counted(ids):
+        total = jnp.zeros(ids.shape, F32)
+        for s in range(n_src):
+            total = total + jnp.where(sources_ref[s : s + 1, :] == ids, 1.0, 0.0)
+        return total
+
+    def as_column(row, width):
+        return jnp.broadcast_to(row, (width, row.shape[1])).T
+
+    inputs[0].wait()
+    for g in range(4):
+        wide = as_column(sends_ref[sides[g]], rows)
+        pick_ref[spans[g]] = jnp.where(
+            wide == lax.broadcasted_iota(jnp.int32, (sent, rows), 1), 1.0, 0.0
+        ).astype(BF16)
+    inputs[1].wait()
+    for i in range(halo // size):
+        wide = as_column(receives_ref[:, i * size : (i + 1) * size], sent)
+        for g in range(4):
+            place_ref[pl.ds(i * size, size), spans[g]] = jnp.where(
+                wide == sides[g] * sent + lax.broadcasted_iota(jnp.int32, (size, sent), 1), 1.0, 0.0
+            ).astype(BF16)
+
+    inputs[2].wait()
+    counts_ref[...] = counted(
+        me * rows + lax.broadcasted_iota(jnp.int32, (rows, columns), 0)
+    ).astype(BF16)
+
+    for copy in inputs[3:]:
         copy.wait()
-
     low_end = jnp.full((1, columns), bounds_ref[0], F32)
     high_end = jnp.full((1, columns), bounds_ref[1], F32)
     centre = (low_end + high_end) / 2.0
@@ -132,31 +159,6 @@
         keeps_ref[k] = damping_next * damping
         gains_ref[k] = 2.0 * damping_next / half_width
         damping = damping_next
-
-    def counted(ids):
-        total = jnp.zeros(ids.shape, F32)
-        for s in range(n_src):
-            total = total + jnp.where(sources_ref[s : s + 1, :] == ids, 1.0, 0.0)
-        return total
-
-    counts_ref[...] = counted(
-        me * rows + lax.broadcasted_iota(jnp.int32, (rows, columns), 0)
-    ).astype(BF16)
-
-    def as_column(row, width):
-        return jnp.broadcast_to(row, (width, row.shape[1])).T
-
-    for g in range(4):
-        wide = as_column(sends_ref[sides[g]], rows)
-        pick_ref[spans[g]] = jnp.where(
-            wide == lax.broadcasted_iota(jnp.int32, (sent, rows), 1), 1.0, 0.0
-        ).astype(BF16)
-    for i in range(halo // size):
-        wide = as_column(receives_ref[:, i * size : (i + 1) * size], sent)
-        for g in range(4):
-            place_ref[pl.ds(i * size, size), spans[g]] = jnp.where(
-                wide == sides[g] * sent + lax.broadcasted_iota(jnp.int32, (size, sent), 1), 1.0, 0.0
-            ).astype(BF16)
 
     eye = lax.broadcasted_iota(jnp.int32, (size, size), 0) == lax.broadcasted_iota(
         jnp.int32, (size, size), 1

time: 48.7 us -> 48.5 us (level)
  no operation moved by 1% of the time
where the time goes in v4:
time: 48.5 us; the launch traced here: 48.3 us
  Pallas kernels  47.7 us (98%)
  between operations  0.64 us (1%)
    pallas_call x1, Pallas kernels, on_device(): pl.pallas_call(functools.partial(kernel, n_patch, n_sub), out_shape=(vmem...  47 us

profile of v4, /device:TPU:0, one launch (start us, length us, event | category | flops | bytes accessed | tf_op | source)
XLA Modules:
  0.0 48.3 jit_solution(18122153333060313274)
XLA Ops:
  0.6 47.0 %chebyshev.1 = (f32[512,128]{1,0:T(8,128)S(1)}, f32[1,128]{1,0:T(1,128)S(1)}) custom-call(s32[2,128]{1,0:T(2,128)} %bitcast.6, f32[4,128]{1,0:T(4,128)} %bitcast.4, f32[4,6,128,128]{3,2,1,0:T(8,128)} %tiles_hbm.1, s32[4,6]{1,0:T(4,128)} %cols_hbm.1, s32[4,1,128]{2,1,0:T(1,128)} %bitcast.5, s32[1,512]{1,0:T(1,128)} %receives_hbm.1, f32[2]{0:T(128)} %bounds_hbm.1), custom_call_target="tpu_custom_call" | custom-call | tf_op jit(solution)/shard_map/chebyshev/pallas_call | solution.py:419
  47.6 0.7 %finish.1 = (f32[512,128]{1,0:T(8,128)}, f32[1,128]{1,0:T(1,128)}) custom-call(f32[512,128]{1,0:T(8,128)S(1)} %get-tuple-element.6.held_ref, f32[1,128]{1,0:T(1,128)S(1)} %get-tuple-element.7.norm_ref), custom_call_target="tpu_custom_call" | custom-call | tf_op jit(solution)/shard_map/finish/pallas_call | solution.py:489
